TPU v7x, 256 devices: a whole 4x4x8 slice. The times are simulated.
256 devices in a mesh: doc: 16 (over y_lo, z), seq: 16 (over x, y_hi, core).
Axes of the slice: x: 4, y: 4 (y_hi: 2, y_lo: 2; y = y_hi * 2 + y_lo), z: 8, core: 2. Of those that a mesh axis runs over, the one named last changes fastest.
Arguments:
- queries: bfloat16 [131072, 512], P(('doc', 'seq')), parts along dimension 0, may hold values from -5 to 5
- teacher_keys: bfloat16 [131072, 128], P(('doc', 'seq')), parts along dimension 0, may hold values from -5 to 5
- teacher_values: bfloat16 [131072, 128], P(('doc', 'seq')), parts along dimension 0, may hold values from -5 to 5
- beacon_starts: int32 [8192], P(('doc', 'seq')), parts along dimension 0, may hold values from 0 to 511, as said below
Outputs:
- output_gap: bfloat16 [131072, 512], P(('doc', 'seq')), parts along dimension 0
- beacon_key_grad: float32 [8192, 128], P(('doc', 'seq')), parts along dimension 0
- beacon_value_grad: float32 [8192, 128], P(('doc', 'seq')), parts along dimension 0
There are 16 independent parts, one for each index of `doc`. A program takes and returns all parts, laid end to end along the dimension named above; each array names one. Nothing has to cross between parts.
Inputs may be any that keep to these rules, and one draw needn't show every extreme that they name: `beacon_starts`: each aligned block of 32 entries belongs to one shard of 512 tokens: its first entry is 0 and its entries rise strictly.
All inputs are finite; a program needn't handle non-finite values.
Results may differ from a plain program's by a relative error of at most 0.009.
Values may be sent and summed in bfloat16 or wider, within the bound.
No kernel may reach another device: no remote copies, remote signals or barrier semaphores. Data moves between devices by JAX's collectives and lax.ppermute only.
A program may use at most 192 MiB of HBM per device.

v0:
```python
import jax
import jax.numpy as jnp
from jax import lax
from jax.sharding import PartitionSpec as P


def sent_to_all(x, axis):
    length = lax.axis_size(axis)
    return lax.all_to_all(jnp.broadcast_to(x[None], (length, *x.shape)), axis, 0, 0, tiled=True)


def joined_along(pieces, dim):
    pieces = jnp.moveaxis(pieces, 0, dim)
    shape = pieces.shape
    return pieces.reshape(*shape[:dim], shape[dim] * shape[dim + 1], *shape[dim + 2 :])


def gather_directly(x, axis, dim):
    pieces = sent_to_all(x, axis)
    return joined_along(pieces, dim)


def cut_along(x, dim, length):
    shape = x.shape
    pieces = x.reshape(*shape[:dim], length, shape[dim] // length, *shape[dim + 1 :])
    return jnp.moveaxis(pieces, dim, 0)


def summed_on_arrival(x, axis, dim):
    length = lax.axis_size(axis)
    pieces = lax.all_to_all(cut_along(x, dim, length), axis, 0, 0, tiled=True)
    return jnp.sum(pieces.astype(jnp.float32), axis=0)


def fresh_state(row_count, head_size):
    return (
        jnp.full((row_count,), -1e30, jnp.float32),
        jnp.zeros((row_count,), jnp.float32),
        jnp.zeros((row_count, head_size), jnp.float32),
    )


def attend_block(state, query_rows, query_pos, piece, head_size, scaling):
    running, total_weight, accum = state
    key_pos = jnp.arange(piece.shape[0], dtype=jnp.int32)
    scores = (
        jnp.dot(query_rows, piece[:, :head_size].T, preferred_element_type=jnp.float32) * scaling
    )
    scores = jnp.where(key_pos[None, :] <= query_pos[:, None], scores, -jnp.inf)
    highest = jnp.maximum(running, jnp.max(scores, axis=1))
    weights = jnp.exp(scores - highest[:, None])
    total_weight = jnp.sum(weights, axis=1)
    accum = jnp.dot(
        weights.astype(jnp.bfloat16), piece[:, head_size:], preferred_element_type=jnp.float32
    )
    return (highest, total_weight, accum)


def guarded(state, query_rows, query_pos, last_pos, piece, start, head_size, scaling):
    return lax.cond(
        start <= last_pos,
        lambda inner: attend_block(inner, query_rows, query_pos, piece, head_size, scaling),
        lambda inner: inner,
        state,
    )


def body(queries, teacher_keys, teacher_values, beacon_starts):
    tok_here, head_size = teacher_keys.shape
    heads = queries.shape[1] // head_size
    seq_index = lax.axis_index("seq")
    scaling = head_size ** (-0.5)
    beac_here = beacon_starts.shape[0]
    joined = jnp.concatenate([teacher_keys, teacher_values], axis=1)
    positions = jnp.arange(tok_here, dtype=jnp.int32)
    endings = jnp.concatenate([beacon_starts[1:], jnp.full((1,), tok_here, jnp.int32)])
    member = (positions[None, :] >= beacon_starts[:, None]) & (
        positions[None, :] < endings[:, None]
    )
    counts = jnp.sum(member.astype(jnp.float32), axis=1)
    pooled = jnp.dot(member.astype(jnp.bfloat16), joined, preferred_element_type=jnp.float32)
    beacon_rows = (pooled / counts[:, None]).astype(jnp.bfloat16)
    beacons = gather_directly(beacon_rows, "seq", 0)
    first_token = seq_index * tok_here
    last_token = first_token + tok_here - 1
    row_count = tok_here * heads
    query_rows = queries.reshape(row_count, head_size)
    local_pos = jnp.arange(row_count, dtype=jnp.int32) // heads
    initial = fresh_state(row_count, head_size)
    folded = guarded(
        initial,
        query_rows,
        first_token + local_pos,
        last_token,
        lax.all_gather(joined, "seq", axis=0, tiled=True),
        jnp.int32(0),
        head_size,
        scaling,
    )
    teacher = folded[2] / folded[1][:, None]
    beacon_count = beacons.shape[0]
    owners = jnp.arange(beacon_count, dtype=jnp.int32) // beac_here
    keys_all = jnp.concatenate([beacons[:, :head_size], teacher_keys], axis=0)
    values_all = jnp.concatenate([beacons[:, head_size:], teacher_values], axis=0)
    visible = jnp.concatenate(
        [
            jnp.broadcast_to(owners[None, :] < seq_index, (row_count, beacon_count)),
            positions[None, :] <= local_pos[:, None],
        ],
        axis=1,
    )
    student_scores = jnp.where(
        visible,
        jnp.dot(query_rows, keys_all.T, preferred_element_type=jnp.float32) * scaling,
        -jnp.inf,
    )
    student_weights = jnp.exp(student_scores - jnp.max(student_scores, axis=1, keepdims=True))
    student_probs = student_weights / jnp.sum(student_weights, axis=1, keepdims=True)
    probs_low = student_probs.astype(jnp.bfloat16)
    student = jnp.dot(probs_low, values_all, preferred_element_type=jnp.float32)
    output_gap = (student - teacher).astype(jnp.bfloat16)
    prob_grad = jnp.dot(output_gap, values_all.T, preferred_element_type=jnp.float32)
    row_dot = jnp.sum(student_probs * prob_grad, axis=1, keepdims=True)
    score_grad = (student_probs * (prob_grad - row_dot)).astype(jnp.bfloat16)
    grad_keys = (
        jnp.dot(score_grad[:, :beacon_count].T, query_rows, preferred_element_type=jnp.float32)
        * scaling
    )
    grad_values = jnp.dot(
        probs_low[:, :beacon_count].T, output_gap, preferred_element_type=jnp.float32
    )
    grads = summed_on_arrival(
        jnp.concatenate([grad_keys, grad_values], axis=1).astype(jnp.bfloat16), "seq", 0
    )
    return (
        output_gap.reshape(tok_here, heads * head_size),
        grads[:, :head_size],
        grads[:, head_size:],
    )


def solution(mesh):
    in_specs = (
        P(("doc", "seq"), None),
        P(("doc", "seq"), None),
        P(("doc", "seq"), None),
        P(("doc", "seq")),
    )
    out_specs = (P(("doc", "seq"), None), P(("doc", "seq"), None), P(("doc", "seq"), None))
    return jax.shard_map(body, mesh=mesh, in_specs=in_specs, out_specs=out_specs, check_vma=False)
```

profile of v0, /device:TPU:1, one launch (start us, length us, event | category | flops | bytes accessed | tf_op | source)
XLA Modules:
  0.0 178.9 jit_solution(6807393799835753735)
XLA Ops:
  7.2 0.0 all-gather.2.cloned.1.call-start
  7.2 0.9 constant_dynamic-update-slice_fusion.1
  8.1 0.9 constant_dynamic-update-slice_fusion
  9.1 0.0 copy-start.1
  9.1 0.7 copy-done.1
  9.8 0.0 all-gather.2.cloned.1.call-update
  9.8 0.7 slice.27
  10.5 0.1 pad_add_fusion
  10.6 0.8 convert_reduce_fusion.1
  11.5 1.2 fusion.29
  12.6 0.7 broadcast_in_dim.24
  13.4 8.4 %all-to-all-start = ((bf16[16,32,256]{2,1,0:T(8,128)(2,1)}), bf16[16,32,256]{2,1,0:T(8,128)(2,1)S(1)}, u32[]{:S(2)}, u32[]{:S(2)}) async-start(bf16[16,32,256]{2,1,0:T(8,128)(2,1)} %broadcast_in_dim.24), calls=%async_computation | async-start | bytes 524288 | tf_op jit(solution)/shard_map/all_to_all | solution.py:9
  21.8 0.6 iota_compare_fusion.1
  22.4 1.4 reshape.61
  23.8 6.8 %all-to-all-done = bf16[16,32,256]{2,1,0:T(8,128)(2,1)S(1)} async-done(((bf16[16,32,256]{2,1,0:T(8,128)(2,1)}), bf16[16,32,256]{2,1,0:T(8,128)(2,1)S(1)}, u32[]{:S(2)}, u32[]{:S(2)}) %all-to-all-start) | async-done | bytes 262176 | tf_op jit(solution)/shard_map/all_to_all | solution.py:9
  30.7 3.3 %fusion.52 = (f32[2048]{0:T(1024)S(1)}, f32[2048,1024]{0,1:T(8,128)S(1)}) fusion(bf16[2048,128]{1,0:T(8,128)(2,1)S(1)} %reshape.61, bf16[512,128]{1,0:T(8,128)(2,1)} %param.7, bf16[512,128]{1,0:T(8,128)(2,1)S(1)} %get-tuple-element.46, pred[2048,512]{0,1:T(32,128)(4,1)S(1)} %iota_compare_fusion.1, pred[1024]{0:T(1024)(128)(4,1)S(1)} %pad.8.clone), kind=kOutput, calls=%fused_computation.74 | convolution fusion | flops 545781760 | bytes 10232832 | tf_op jit(solution)/shard_map/dot_general | solution.py:114
  34.0 1.2 fusion.13
  35.2 5.4 %fusion.48 = (bf16[2048,1024]{0,1:T(8,128)(2,1)}, f32[2048,1024]{0,1:T(8,128)}) fusion(f32[2048]{0:T(1024)S(1)} %fusion.13, f32[2048,1024]{0,1:T(8,128)S(1)} %get-tuple-element.50, f32[2048]{0:T(1024)S(1)} %get-tuple-element.49), kind=kLoop, calls=%fused_computation.71 | loop fusion | flops 6291456 | bytes 20987904 | tf_op jit(solution)/shard_map/convert_element_type | solution.py:119
  40.5 36.3 %all-gather.2.cloned.1.call-done = bf16[8192,256]{1,0:T(8,128)(2,1)} async-done(((bf16[512,256]{1,0:T(8,128)(2,1)}), bf16[8192,256]{1,0:T(8,128)(2,1)}) %all-gather.2.cloned.1.call-update) | async-done | bytes 4194320 | tf_op jit(solution)/shard_map/all_gather | solution.py:95
  76.8 0.0 copy-start.2
  76.8 73.1 %conditional.1 = (f32[2048]{0:T(1024)S(1)}, f32[2048,128]{1,0:T(8,128)S(1)}) conditional(s32[]{:T(128)} %convert_element_type.30, () %tuple.16, (s32[]{:T(128)}, s32[2048]{0:T(1024)S(1)}, s32[2048]{0:T(1024)S(1)}, bf16[8192,256]{1,0:T(8,128)(2,1)}, bf16[2048,128]{1,0:T(8,128)(2,1)S(1)}) %tuple.17), branch_computations={%region_3.4_spmd, %region_4.0_spmd} | conditional | flops 8824829952 | bytes 207192080 | solution.py:60
  76.8 25.5 %fusion.2 = (f32[2048]{0:T(1024)S(1)}, f32[2048,8192]{1,0:T(8,128)}) fusion(s32[2048]{0:T(1024)S(1)} %fusion.8, bf16[2048,128]{1,0:T(8,128)(2,1)S(1)} %get-tuple-element.32, bf16[8192,256]{1,0:T(8,128)(2,1)} %get-tuple-element.33), kind=kOutput, calls=%fused_computation.5 | convolution fusion | flops 4362074112 | bytes 69746688 | tf_op jit(solution)/shard_map/cond/branch_1_fun/dot_general | solution.py:47
  102.3 25.6 %fusion.3 = f32[2048,128]{1,0:T(8,128)S(1)} fusion(f32[2048,8192]{1,0:T(8,128)} %get-tuple-element.44, f32[2048]{0:T(1024)S(1)} %broadcast_maximum_fusion, s32[2048]{0:T(1024)S(1)} %fusion.8, bf16[8192,256]{1,0:T(8,128)(2,1)} %get-tuple-element.33), kind=kOutput, calls=%fused_computation.6 | convolution fusion | flops 4378853376 | bytes 70270976 | tf_op jit(solution)/shard_map/cond/branch_1_fun/dot_general | solution.py:53
  127.9 22.0 %fusion.1 = f32[2048]{0:T(1024)S(1)} fusion(f32[2048,8192]{1,0:T(8,128)} %get-tuple-element.44, f32[2048]{0:T(1024)S(1)} %broadcast_maximum_fusion, s32[2048]{0:T(1024)S(1)} %fusion.8), kind=kLoop, calls=%fused_computation.4 | loop fusion | flops 83884032 | bytes 67133440 | tf_op jit(solution)/shard_map/cond/branch_1_fun/reduce_sum | solution.py:52
  150.0 0.0 copy-start
  150.0 0.0 slice-start
  150.0 0.0 copy-done.2
  150.0 0.0 slice-start.1
  150.0 3.8 %fusion.15 = bf16[2048,128]{1,0:T(8,128)(2,1)S(1)} fusion(bf16[2048,1024]{0,1:T(8,128)(2,1)} %get-tuple-element.41, f32[2048,128]{1,0:T(8,128)S(1)} %get-tuple-element.39, f32[2048]{0:T(1024)S(1)} %get-tuple-element.40, bf16[512,128]{1,0:T(8,128)(2,1)S(1)} %copy-done.2, bf16[512,128]{1,0:T(8,128)(2,1)S(1)} %get-tuple-element.45), kind=kOutput, calls=%fused_computation.28 | convolution fusion | flops 538181632 | bytes 6037504 | tf_op jit(solution)/shard_map/dot_general | solution.py:120
  153.8 0.0 copy-done
  153.8 0.7 fusion.23
  154.5 0.1 slice-done
  154.7 1.2 slice-done.1
  155.9 1.3 multiply_reduce_fusion
  157.2 0.7 fusion.26
  157.9 0.7 pad_maximum_fusion.1
  158.6 3.9 %all-to-all-start.1 = ((bf16[16,32,256]{2,1,0:T(8,128)(2,1)}), bf16[16,32,256]{2,1,0:T(8,128)(2,1)S(1)}, u32[]{:S(2)}, u32[]{:S(2)}) async-start(bf16[16,32,256]{2,1,0:T(8,128)(2,1)} %pad_maximum_fusion.1), calls=%async_computation.1 | async-start | bytes 524288 | tf_op jit(solution)/shard_map/all_to_all | solution.py:31
  162.5 1.1 reshape.62
  163.7 7.8 %all-to-all-done.1 = bf16[16,32,256]{2,1,0:T(8,128)(2,1)S(1)} async-done(((bf16[16,32,256]{2,1,0:T(8,128)(2,1)}), bf16[16,32,256]{2,1,0:T(8,128)(2,1)S(1)}, u32[]{:S(2)}, u32[]{:S(2)}) %all-to-all-start.1) | async-done | bytes 262176 | tf_op jit(solution)/shard_map/all_to_all | solution.py:31
  171.5 0.6 fusion.51
  (10 shorter events, 0.1 us)
Async XLA Ops:
  7.2 69.7 %all-gather.2.cloned.1.call-start = ((), (), s32[]{:S(2)}) async-start(), calls=%async_computation.2 | async-start | bytes 4456448 | tf_op jit(solution)/shard_map/all_gather | solution.py:95
  9.1 0.7 copy-start.1
  13.4 17.3 %all-to-all-start = ((bf16[16,32,256]{2,1,0:T(8,128)(2,1)}), bf16[16,32,256]{2,1,0:T(8,128)(2,1)S(1)}, u32[]{:S(2)}, u32[]{:S(2)}) async-start(bf16[16,32,256]{2,1,0:T(8,128)(2,1)} %broadcast_in_dim.24), calls=%async_computation | async-start | bytes 524288 | tf_op jit(solution)/shard_map/all_to_all | solution.py:9
  76.8 73.2 %copy-start.2 = (bf16[512,128]{1,0:T(8,128)(2,1)S(1)}, bf16[512,128]{1,0:T(8,128)(2,1)}, u32[]{:S(2)}) copy-start(bf16[512,128]{1,0:T(8,128)(2,1)} %param.8) | copy-start | bytes 393220
  150.0 3.9 %copy-start = (bf16[2048,1024]{0,1:T(8,128)(2,1)S(1)}, bf16[2048,1024]{0,1:T(8,128)(2,1)}, u32[]{:S(2)}) copy-start(bf16[2048,1024]{0,1:T(8,128)(2,1)} %get-tuple-element.41) | copy-start | bytes 12582916
  150.0 4.7 %slice-start = ((s8[8388608]{0:T(1024)(128)(4,1)}), s8[4194304]{0:T(1024)(128)(4,1)S(1)}, s32[]{:S(2)}) async-start(s8[8388608]{0:T(1024)(128)(4,1)} %bitcast.12), calls=%async_computation.3 | async-start | bytes 8388608
  150.0 5.9 %slice-start.1 = ((s8[8388608]{0:T(1024)(128)(4,1)}), s8[4194304]{0:T(1024)(128)(4,1)S(1)}, s32[]{:S(2)}) async-start(s8[8388608]{0:T(1024)(128)(4,1)} %bitcast.12), calls=%async_computation.4 | async-start | bytes 8388608
  158.6 12.8 %all-to-all-start.1 = ((bf16[16,32,256]{2,1,0:T(8,128)(2,1)}), bf16[16,32,256]{2,1,0:T(8,128)(2,1)S(1)}, u32[]{:S(2)}, u32[]{:S(2)}) async-start(bf16[16,32,256]{2,1,0:T(8,128)(2,1)} %pad_maximum_fusion.1), calls=%async_computation.1 | async-start | bytes 524288 | tf_op jit(solution)/shard_map/all_to_all | solution.py:31
Sparse Core Ops, SparseCore 0:
  11.2 65.5 all-gather.1
where the time goes:
time: 179 us
  matrix products  62 us (35%)
  waiting for transfers between devices  50.9 us (28%)
  other arithmetic  30.9 us (17%)
  between operations  14.2 us (8%)
  starting transfers between devices  12.4 us (7%)
  local copies, waits for them, and re-layouts  8.47 us (5%)
    all_gather x1, waiting for transfers between devices, body(): lax.all_gather(joined, 'seq', axis=0, tiled=True)  36.3 us
    dot_general x1, matrix products, attend_block(): jnp.dot(weights.astype(jnp.bfloat16), piece[:, head_size:], preferred_ele...  25.6 us
    dot_general x1, matrix products, attend_block(): jnp.dot(query_rows, piece[:, :head_size].T, preferred_element_type=jnp.fl...  25.5 us
    reduce_sum x1, other arithmetic, attend_block(): total_weight = jnp.sum(weights, axis=1)  22 us
    all_to_all x1, starting transfers between devices, sent_to_all(): lax.all_to_all(jnp.broadcast_to(x[None], (length, *x.shape)), axis, 0, 0,...  8.44 us
    all_to_all x1, waiting for transfers between devices, summed_on_arrival(): pieces = lax.all_to_all(cut_along(x, dim, length), axis, 0, 0, tiled=True)  7.76 us
    all_to_all x1, waiting for transfers between devices, sent_to_all(): lax.all_to_all(jnp.broadcast_to(x[None], (length, *x.shape)), axis, 0, 0,...  6.83 us
    convert_element_type x1, other arithmetic, body(): probs_low = student_probs.astype(jnp.bfloat16)  5.39 us
  transfers between devices with their start and end apart: 3, of which 3 were waited for; matrix products, arithmetic and copies ran while one was open for 9% of the time, Pallas kernels for 0%

commit v1 on v0

--- a/solution.py
+++ b/solution.py
@@ -2,6 +2,13 @@
 import jax.numpy as jnp
 from jax import lax
 from jax.sharding import PartitionSpec as P
+
+
+def gather_over(shard, axis, d):
+    n_dev = lax.axis_size(axis)
+    blocks = jnp.stack([shard for _ in range(n_dev)])
+    blocks = lax.all_to_all(blocks, axis, split_axis=0, concat_axis=0)
+    return jnp.concatenate(blocks, axis=d)
 
 
 def sent_to_all(x, axis):
@@ -92,7 +99,7 @@
         query_rows,
         first_token + local_pos,
         last_token,
-        lax.all_gather(joined, "seq", axis=0, tiled=True),
+        gather_over(joined, "seq", 0),
         jnp.int32(0),
         head_size,
         scaling,

time: 179 us -> 186 us (1.039)
  blocking collectives: 0 us -> 17.1 us
  between operations: 14.2 us -> 0.81 us
  starting transfers between devices: 12.4 us -> 17.2 us
  matrix products: 62 us -> 60.1 us
    all_to_all x1, waiting for transfers between devices: 6.83 us -> 43.5 us  [gather_over(): blocks = lax.all_to_all(blocks, axis, split_axis=0, concat_axis=0)]
    all_gather x1 -> x0, waiting for transfers between devices: 36.3 us -> none  [body(): lax.all_gather(joined, 'seq', axis=0, tiled=True)]
    all_to_all x0 -> x1, blocking collectives: none -> 17.1 us  [sent_to_all(): lax.all_to_all(jnp.broadcast_to(x[None], (length, *x.shape)), axis, 0, 0,...]
    all_to_all x1, starting transfers between devices: 3.94 us -> 12.5 us  [summed_on_arrival(): pieces = lax.all_to_all(cut_along(x, dim, length), axis, 0, 0, tiled=True)]
    all_to_all x1, starting transfers between devices: 8.44 us -> 4.67 us  [gather_over(): blocks = lax.all_to_all(blocks, axis, split_axis=0, concat_axis=0)]
    another operation x0 -> x1, local copies, waits for them, and re-layouts: none -> 2.33 us  [gather_over(): blocks = jnp.stack([shard for _ in range(n_dev)])]
  transfers between devices with their start and end apart: 3 -> 2, of which waited for: 3 -> 2; matrix products, arithmetic and copies ran while one was open for 9% -> 5% of each run, Pallas kernels for 0% -> 0%
where the time goes in v1:
time: 186 us
  matrix products  60.1 us (32%)
  waiting for transfers between devices  51.2 us (28%)
  other arithmetic  30.9 us (17%)
  starting transfers between devices  17.2 us (9%)
  blocking collectives  17.1 us (9%)
  local copies, waits for them, and re-layouts  8.45 us (5%)
    all_to_all x1, waiting for transfers between devices, gather_over(): blocks = lax.all_to_all(blocks, axis, split_axis=0, concat_axis=0)  43.5 us
    dot_general x1, matrix products, attend_block(): jnp.dot(weights.astype(jnp.bfloat16), piece[:, head_size:], preferred_ele...  25.6 us
    dot_general x1, matrix products, attend_block(): jnp.dot(query_rows, piece[:, :head_size].T, preferred_element_type=jnp.fl...  25.5 us
    reduce_sum x1, other arithmetic, attend_block(): total_weight = jnp.sum(weights, axis=1)  22 us
    all_to_all x1, blocking collectives, sent_to_all(): lax.all_to_all(jnp.broadcast_to(x[None], (length, *x.shape)), axis, 0, 0,...  17.1 us
    all_to_all x1, starting transfers between devices, summed_on_arrival(): pieces = lax.all_to_all(cut_along(x, dim, length), axis, 0, 0, tiled=True)  12.5 us
    all_to_all x1, waiting for transfers between devices, summed_on_arrival(): pieces = lax.all_to_all(cut_along(x, dim, length), axis, 0, 0, tiled=True)  7.76 us
    convert_element_type x1, other arithmetic, body(): probs_low = student_probs.astype(jnp.bfloat16)  5.3 us
  transfers between devices with their start and end apart: 2, of which 2 were waited for; matrix products, arithmetic and copies ran while one was open for 5% of the time, Pallas kernels for 0%

profile of v1, /device:TPU:1, one launch (start us, length us, event | category | flops | bytes accessed | tf_op | source)
XLA Modules:
  0.0 185.7 jit_solution(17196813131044252290)
XLA Ops:
  0.6 0.0 copy-start.2
  0.6 0.8 slice.27
  1.4 0.1 pad_add_fusion
  1.5 0.8 convert_reduce_fusion.1
  2.3 0.9 constant_dynamic-update-slice_fusion.1
  3.3 0.9 constant_dynamic-update-slice_fusion
  4.2 0.0 copy-start.3
  4.2 0.9 fusion.29
  5.2 17.1 %all_to_all.15 = bf16[16,32,256]{2,1,0:T(8,128)(2,1)S(1)} all-to-all(bf16[16,32,256]{2,1,0:T(8,128)(2,1)S(1)} %broadcast_in_dim.24), channel_id=1, replica_groups=mesh['doc'=16,'seq'=16] {'seq'}, dimensions={0} | all-to-all | bytes 524288 | tf_op jit(solution)/shard_map/all_to_all | solution.py:16
  22.3 2.3 %stack.2 = bf16[16,512,256]{2,1,0:T(8,128)(2,1)} broadcast(bf16[512,256]{1,0:T(8,128)(2,1)S(1)} %constant_dynamic-update-slice_fusion), dimensions={1,2} | broadcast | bytes 4456448 | tf_op jit(solution)/shard_map/stack | solution.py:9
  24.6 4.7 %all-to-all-start.1 = ((bf16[16,512,256]{2,1,0:T(8,128)(2,1)}), bf16[16,512,256]{2,1,0:T(8,128)(2,1)}, u32[]{:S(2)}, u32[]{:S(2)}) async-start(bf16[16,512,256]{2,1,0:T(8,128)(2,1)} %stack.2), calls=%async_computation.1 | async-start | bytes 8388608 | tf_op jit(solution)/shard_map/all_to_all | solution.py:10
  29.3 0.0 copy-done.2
  29.3 0.3 reshape.67
  29.6 0.6 iota_compare_fusion.1
  30.3 0.0 copy-done.3
  30.3 1.6 fusion.52
  31.9 1.2 fusion.13
  33.1 5.3 %fusion.48 = (bf16[2048,1024]{0,1:T(8,128)(2,1)}, f32[2048,1024]{0,1:T(8,128)}) fusion(f32[2048]{0:T(1024)S(1)} %fusion.13, f32[2048,1024]{0,1:T(8,128)S(1)} %get-tuple-element.51, f32[2048]{0:T(1024)S(1)} %get-tuple-element.50), kind=kLoop, calls=%fused_computation.71 | loop fusion | flops 6291456 | bytes 20987904 | tf_op jit(solution)/shard_map/convert_element_type | solution.py:126
  38.4 43.5 %all-to-all-done.1 = bf16[16,512,256]{2,1,0:T(8,128)(2,1)} async-done(((bf16[16,512,256]{2,1,0:T(8,128)(2,1)}), bf16[16,512,256]{2,1,0:T(8,128)(2,1)}, u32[]{:S(2)}, u32[]{:S(2)}) %all-to-all-start.1) | async-done | bytes 4194336 | tf_op jit(solution)/shard_map/all_to_all | solution.py:10
  81.9 0.0 copy-start.1
  81.9 73.1 %conditional.1 = (f32[2048]{0:T(1024)S(1)}, f32[2048,128]{1,0:T(8,128)S(1)}) conditional(s32[]{:T(128)} %convert_element_type.30, () %tuple.16, (s32[]{:T(128)}, s32[2048]{0:T(1024)S(1)}, s32[2048]{0:T(1024)S(1)}, bf16[16,512,256]{2,1,0:T(8,128)(2,1)}, bf16[2048,128]{1,0:T(8,128)(2,1)S(1)}) %tuple.17), branch_computations={%region_3.4_spmd, %region_4.0_spmd} | conditional | flops 8824829952 | bytes 207192080 | solution.py:67
  81.9 25.5 %fusion.2 = (f32[2048]{0:T(1024)S(1)}, f32[2048,8192]{1,0:T(8,128)}) fusion(s32[2048]{0:T(1024)S(1)} %fusion.8, bf16[2048,128]{1,0:T(8,128)(2,1)S(1)} %get-tuple-element.33, bf16[8192,256]{1,0:T(8,128)(2,1)} %bitcast), kind=kOutput, calls=%fused_computation.5 | convolution fusion | flops 4362074112 | bytes 69746688 | tf_op jit(solution)/shard_map/cond/branch_1_fun/dot_general | solution.py:54
  107.4 25.6 %fusion.3 = f32[2048,128]{1,0:T(8,128)S(1)} fusion(f32[2048,8192]{1,0:T(8,128)} %get-tuple-element.45, f32[2048]{0:T(1024)S(1)} %broadcast_maximum_fusion, s32[2048]{0:T(1024)S(1)} %fusion.8, bf16[8192,256]{1,0:T(8,128)(2,1)} %bitcast), kind=kOutput, calls=%fused_computation.6 | convolution fusion | flops 4378853376 | bytes 70270976 | tf_op jit(solution)/shard_map/cond/branch_1_fun/dot_general | solution.py:60
  133.0 22.0 %fusion.1 = f32[2048]{0:T(1024)S(1)} fusion(f32[2048,8192]{1,0:T(8,128)} %get-tuple-element.45, f32[2048]{0:T(1024)S(1)} %broadcast_maximum_fusion, s32[2048]{0:T(1024)S(1)} %fusion.8), kind=kLoop, calls=%fused_computation.4 | loop fusion | flops 83884032 | bytes 67133440 | tf_op jit(solution)/shard_map/cond/branch_1_fun/reduce_sum | solution.py:59
  155.0 0.0 copy-start
  155.0 0.0 slice-start
  155.0 0.0 copy-done.1
  155.1 0.0 slice-start.1
  155.1 3.8 %fusion.15 = bf16[2048,128]{1,0:T(8,128)(2,1)S(1)} fusion(bf16[2048,1024]{0,1:T(8,128)(2,1)} %get-tuple-element.42, f32[2048,128]{1,0:T(8,128)S(1)} %get-tuple-element.40, f32[2048]{0:T(1024)S(1)} %get-tuple-element.41, bf16[512,128]{1,0:T(8,128)(2,1)S(1)} %copy-done.1, bf16[512,128]{1,0:T(8,128)(2,1)S(1)} %get-tuple-element.46), kind=kOutput, calls=%fused_computation.28 | convolution fusion | flops 538181632 | bytes 6037504 | tf_op jit(solution)/shard_map/dot_general | solution.py:127
  158.9 0.0 copy-done
  158.9 0.7 fusion.23
  159.6 0.2 slice-done
  159.8 1.2 slice-done.1
  161.0 1.3 multiply_reduce_fusion
  162.2 0.7 fusion.26
  162.9 0.7 pad_maximum_fusion.1
  163.7 12.5 %all-to-all-start.2 = ((bf16[16,32,256]{2,1,0:T(8,128)(2,1)}), bf16[16,32,256]{2,1,0:T(8,128)(2,1)S(1)}, u32[]{:S(2)}, u32[]{:S(2)}) async-start(bf16[16,32,256]{2,1,0:T(8,128)(2,1)} %pad_maximum_fusion.1), calls=%async_computation.2 | async-start | bytes 524288 | tf_op jit(solution)/shard_map/all_to_all | solution.py:38
  176.2 1.1 reshape.68
  177.3 7.8 %all-to-all-done.2 = bf16[16,32,256]{2,1,0:T(8,128)(2,1)S(1)} async-done(((bf16[16,32,256]{2,1,0:T(8,128)(2,1)}), bf16[16,32,256]{2,1,0:T(8,128)(2,1)S(1)}, u32[]{:S(2)}, u32[]{:S(2)}) %all-to-all-start.2) | async-done | bytes 262176 | tf_op jit(solution)/shard_map/all_to_all | solution.py:38
  185.1 0.6 fusion.51
  (11 shorter events, 0.1 us)
Async XLA Ops:
  0.6 28.6 %copy-start.2 = (bf16[512,512]{1,0:T(8,128)(2,1)S(1)}, bf16[512,512]{1,0:T(8,128)(2,1)}, u32[]{:S(2)}) copy-start(bf16[512,512]{1,0:T(8,128)(2,1)} %param.6) | copy-start | bytes 1572868
  4.2 26.1 %copy-start.3 = (bf16[512,128]{1,0:T(8,128)(2,1)S(1)}, bf16[512,128]{1,0:T(8,128)(2,1)}, u32[]{:S(2)}) copy-start(bf16[512,128]{1,0:T(8,128)(2,1)} %param.7) | copy-start | bytes 393220
  24.6 57.3 %all-to-all-start.1 = ((bf16[16,512,256]{2,1,0:T(8,128)(2,1)}), bf16[16,512,256]{2,1,0:T(8,128)(2,1)}, u32[]{:S(2)}, u32[]{:S(2)}) async-start(bf16[16,512,256]{2,1,0:T(8,128)(2,1)} %stack.2), calls=%async_computation.1 | async-start | bytes 8388608 | tf_op jit(solution)/shard_map/all_to_all | solution.py:10
  81.9 73.2 %copy-start.1 = (bf16[512,128]{1,0:T(8,128)(2,1)S(1)}, bf16[512,128]{1,0:T(8,128)(2,1)}, u32[]{:S(2)}) copy-start(bf16[512,128]{1,0:T(8,128)(2,1)} %param.8) | copy-start | bytes 393220
  155.0 3.9 %copy-start = (bf16[2048,1024]{0,1:T(8,128)(2,1)S(1)}, bf16[2048,1024]{0,1:T(8,128)(2,1)}, u32[]{:S(2)}) copy-start(bf16[2048,1024]{0,1:T(8,128)(2,1)} %get-tuple-element.42) | copy-start | bytes 12582916
  155.0 4.7 %slice-start = ((s8[8388608]{0:T(1024)(128)(4,1)}), s8[4194304]{0:T(1024)(128)(4,1)S(1)}, s32[]{:S(2)}) async-start(s8[8388608]{0:T(1024)(128)(4,1)} %bitcast.13), calls=%async_computation.3 | async-start | bytes 8388608
  155.1 5.9 %slice-start.1 = ((s8[8388608]{0:T(1024)(128)(4,1)}), s8[4194304]{0:T(1024)(128)(4,1)S(1)}, s32[]{:S(2)}) async-start(s8[8388608]{0:T(1024)(128)(4,1)} %bitcast.13), calls=%async_computation.4 | async-start | bytes 8388608
  163.7 21.4 %all-to-all-start.2 = ((bf16[16,32,256]{2,1,0:T(8,128)(2,1)}), bf16[16,32,256]{2,1,0:T(8,128)(2,1)S(1)}, u32[]{:S(2)}, u32[]{:S(2)}) async-start(bf16[16,32,256]{2,1,0:T(8,128)(2,1)} %pad_maximum_fusion.1), calls=%async_computation.2 | async-start | bytes 524288 | tf_op jit(solution)/shard_map/all_to_all | solution.py:38
